TPU v7x, 32 devices: a whole 2x2x4 slice. The times are simulated.
32 devices in a mesh: seq: 8 (over z, y), mp: 4 (over x, core).
Axes of the slice: x: 2, y: 2, z: 4, core: 2. Of those that a mesh axis runs over, the one named last changes fastest.
Arguments:
- gate_in: bfloat16 [8192, 1024], P('seq', 'mp'), may hold values from -5 to 5
- value_in: bfloat16 [8192, 1024], P('seq', 'mp'), may hold values from -5 to 5
- out_gate: bfloat16 [8192, 1024], P('seq', 'mp'), may hold values from -10 to 10
- filter_taps: bfloat16 [4096, 1024], P('seq', 'mp'), may hold values from -0.09375 to 0.09375
- skip_gain: float32 [1024], P('mp'), may hold values from -4 to 4
Outputs:
- output: bfloat16 [8192, 1024], P('seq', 'mp')
All inputs are finite; a program needn't handle non-finite values.
Results may differ from a plain program's by a relative error of at most 0.009.
Values may be sent and summed in bfloat16 or wider, within the bound.
A program may use at most 64 MiB of HBM per device.

v0:
```python
import functools

import jax
import jax.numpy as jnp
from jax import lax
from jax.experimental import pallas as pl
from jax.experimental.pallas import tpu as pltpu
from jax.sharding import PartitionSpec as P

MESH = pl.DeviceIdType.MESH
LANES = 128
TAPS, GATED, RESULT = 0, 1, 2
EPS = 1e-05


def peer_of(me, k, n):
    if n & (n - 1) == 0:
        return me ^ k
    return lax.rem(me + k, n)


def source_of(me, k, n):
    if n & (n - 1) == 0:
        return me ^ k
    return lax.rem(me + n - k, n)


def kernel(cfg, gate_in, value_in, og_in, taps_in, skip_in, out, gate, value, og, taps, skip, stage,
           xm, hm, xr, hr, hf, xpad, rs, cr, ogt, mixed, power, powers, load_sem, send_sem, recv_sem,
           own_sem, psend_sem, precv_sem):
    n, m, channels, blocks, cl, width, groups, sent_taps, hs, he, total_c = cfg
    me = lax.axis_index("seq")
    mine = lax.axis_index("mp")
    nd = hs * he
    order = list(range(n - 1, 0, -1))

    loads = [
        pltpu.make_async_copy(src, dst, load_sem.at[i])
        for i, (src, dst) in enumerate(
            [(taps_in, taps), (gate_in, gate), (value_in, value), (og_in, og), (skip_in, skip)]
        )
    ]
    for load in loads:
        load.start()

    barrier = pltpu.get_barrier_semaphore()
    for k in range(1, n):
        pl.semaphore_signal(barrier, inc=1, device_id={"seq": peer_of(me, k, n)}, device_id_type=MESH)
    for k in range(1, m):
        pl.semaphore_signal(barrier, inc=1, device_id={"mp": peer_of(mine, k, m)}, device_id_type=MESH)

    loads[0].wait()
    if sent_taps:
        for e in range(he):
            part = taps[e * LANES:(e + 1) * LANES, :].astype(jnp.float32)
            stage[pl.ds(e, channels, stride=he), :] = part.T
        hm[...] = stage[: channels * he, :].astype(jnp.bfloat16).reshape(hm.shape)
    loads[1].wait()
    loads[2].wait()
    for a in range(blocks):
        span = slice(a * LANES, (a + 1) * LANES)
        part = gate[span, :].astype(jnp.float32) * value[span, :].astype(jnp.float32)
        stage[pl.ds(a, channels, stride=blocks), :] = part.T
    xm[...] = stage[...].astype(jnp.bfloat16).reshape(xm.shape)

    pl.semaphore_wait(barrier, n - 1 + m - 1)

    def rows_of(kind, g):
        per = he if kind == TAPS else blocks
        return pl.ds(g * width * per, width * per)

    def refs(kind):
        return {TAPS: (hm, hr), GATED: (xm, xr), RESULT: (rs, cr)}[kind]

    def remote(kind, g, k):
        src, dst = refs(kind)
        to = peer_of(me, k, n)
        rows = rows_of(kind, g)
        return pltpu.make_async_remote_copy(
            src_ref=src.at[to, rows],
            dst_ref=dst.at[me, rows],
            send_sem=send_sem.at[kind, g, k],
            recv_sem=recv_sem.at[kind, g, k],
            device_id={"seq": to},
            device_id_type=MESH,
        )

    def arrival(kind, g, k):
        src, dst = refs(kind)
        whence = source_of(me, k, n)
        rows = rows_of(kind, g)
        return pltpu.make_async_remote_copy(
            src_ref=src.at[whence, rows],
            dst_ref=dst.at[whence, rows],
            send_sem=send_sem.at[kind, g, k],
            recv_sem=recv_sem.at[kind, g, k],
            device_id={"seq": whence},
            device_id_type=MESH,
        )

    def own(kind, g):
        src, dst = refs(kind)
        rows = rows_of(kind, g)
        return pltpu.make_async_copy(src.at[me, rows], dst.at[me, rows], own_sem.at[kind, g])

    forward = ([TAPS] if sent_taps else []) + [GATED]
    for g in range(groups):
        for kind in forward:
            for k in order:
                remote(kind, g, k).start()
            own(kind, g).start()

    loads[3].wait()
    loads[4].wait()
    for a in range(blocks):
        span = slice(a * LANES, (a + 1) * LANES)
        ogt[pl.ds(a, channels, stride=blocks), :] = og[span, :].astype(jnp.float32).T
    xpad[:, :nd, :] = jnp.zeros((2, nd, LANES), jnp.float32)

    lane = lax.broadcasted_iota(jnp.int32, (16, LANES), 1)
    sub = lax.broadcasted_iota(jnp.int32, (16, LANES), 0)
    total = n * blocks

    def toeplitz(c):
        lines = []
        for d in range(nd):
            source = hf if sent_taps else taps
            line = source[d // he, pl.ds(c * he + d % he, 1), :]
            line = jnp.broadcast_to(line, (16, LANES))
            lines.append(pltpu.roll(line, 0, 1, stride=1, stride_axis=0))
        zero = jnp.zeros((16, LANES), jnp.float32)
        first = []
        for d in range(nd + 1):
            here = lines[d] if d < nd else zero
            before = lines[d - 1] if d > 0 else zero
            first.append(jnp.where(lane >= sub, here, before).astype(jnp.bfloat16))
        none = jnp.zeros((16, LANES), jnp.bfloat16)
        tiles = []
        turned = [[(f if q == 0 else pltpu.roll(f, 16 * q, 1)) for q in range(8)] for f in first]
        for d in range(nd + 1):
            rows = []
            for q in range(8):
                before = turned[d - 1][q] if d > 0 else none
                rows.append(turned[d][q] if q == 0 else jnp.where(lane >= 16 * q, turned[d][q], before))
            tiles.append(jnp.concatenate(rows, axis=0))
        return tiles

    def one_pair(base, p):
        c0 = base + 2 * p
        start = pl.multiple_of(c0 * blocks, 2 * blocks)
        both = xr[:, pl.ds(start, 2 * blocks), :].astype(jnp.float32)
        results = []
        for e in range(2):
            rows = both[:, e * blocks:(e + 1) * blocks, :].reshape(total, LANES)
            xpad[e, nd:, :] = rows
            tiles = toeplitz(c0 + e)
            acc = rows * skip[me * cl + c0 + e]
            for d in range(0, nd + 1, 2):
                ds = [d, d + 1] if d + 1 <= nd else [d]
                left = [xpad[e, nd - x:nd - x + total, :].astype(jnp.bfloat16) for x in ds]
                left = left[0] if len(ds) == 1 else jnp.concatenate(left, axis=1)
                right = tiles[d] if len(ds) == 1 else jnp.concatenate([tiles[d], tiles[d + 1]], axis=0)
                acc = acc + jnp.dot(left, right, preferred_element_type=jnp.float32)
            results.append(acc.reshape(n, blocks, LANES))
        rs[:, pl.ds(start, 2 * blocks), :] = jnp.concatenate(results, axis=1).astype(jnp.bfloat16)

    for g in range(groups):
        for kind in forward:
            own(kind, g).wait()
            for k in order:
                arrival(kind, g, k).wait_recv()
        if sent_taps:
            rows = rows_of(TAPS, g)
            hf[:, rows, :] = hr[:, rows, :].astype(jnp.float32)

        def step(p, carry):
            one_pair(g * width, p)
            return carry

        lax.fori_loop(0, width // 2, step, 0)
        for k in order:
            remote(RESULT, g, k).start()
        own(RESULT, g).start()

    power[...] = jnp.zeros_like(power)
    for g in range(groups):
        own(RESULT, g).wait()
        for k in order:
            arrival(RESULT, g, k).wait_recv()

        def gather(d, carry):
            rows = rows_of(RESULT, g)
            at = pl.multiple_of(d * cl * blocks + g * width * blocks, width * blocks)
            piece = ogt[pl.ds(at, width * blocks), :] * cr[d, rows, :].astype(jnp.float32)
            mixed[pl.ds(at, width * blocks), :] = piece
            square = (piece * piece).reshape(width, blocks, LANES)
            power[...] += jnp.sum(square, axis=0)
            return carry

        lax.fori_loop(0, n, gather, 0)

    def exchange(k, incoming):
        other = source_of(mine, k, m) if incoming else peer_of(mine, k, m)
        return pltpu.make_async_remote_copy(
            src_ref=power,
            dst_ref=powers.at[other if incoming else mine],
            send_sem=psend_sem.at[k],
            recv_sem=precv_sem.at[k],
            device_id={"mp": other},
            device_id_type=MESH,
        )

    for k in range(1, m):
        exchange(k, False).start()
    for kind in forward + [RESULT]:
        for g in range(groups):
            for k in order:
                remote(kind, g, k).wait_send()
    for k in range(1, m):
        exchange(k, True).wait_recv()
    sums = power[...]
    for k in range(1, m):
        sums = sums + powers[source_of(mine, k, m)]
    scale = 1.0 / jnp.sqrt(sums / total_c + EPS)
    for a in range(blocks):
        part = mixed[pl.ds(a, channels, stride=blocks), :] * scale[a:a + 1, :]
        out[a * LANES:(a + 1) * LANES, :] = part.T.astype(jnp.bfloat16)
    for k in range(1, m):
        exchange(k, False).wait_send()


def solution(mesh):
    n, m = mesh.shape["seq"], mesh.shape["mp"]

    def local(gate_in, value_in, out_gate, filter_taps, skip_gain):
        tokens, channels = gate_in.shape
        blocks = tokens // LANES
        cl = channels // n
        width = min(cl, 8)
        groups = cl // width
        own_taps = filter_taps.shape[0]
        sent_taps = own_taps % LANES == 0 and (width * (own_taps // LANES)) % 16 == 0
        nd = own_taps * n // LANES
        if sent_taps:
            hs, he, taps = n, own_taps // LANES, filter_taps
        else:
            hs, he = 1, nd
            moved = lax.all_to_all(filter_taps, "seq", split_axis=1, concat_axis=0, tiled=True)
            taps = moved.astype(jnp.float32).T.reshape(1, cl * nd, LANES)
        cfg = (n, m, channels, blocks, cl, width, groups, sent_taps, hs, he, channels * m)
        vmem = pl.BlockSpec(memory_space=pltpu.VMEM)
        message = (n, cl * blocks, LANES)
        taps_message = (n, cl * he, LANES) if sent_taps else (n, 16, LANES)
        return pl.pallas_call(
            functools.partial(kernel, cfg),
            out_shape=jax.ShapeDtypeStruct((tokens, channels), jnp.bfloat16),
            in_specs=[pl.BlockSpec(memory_space=pltpu.HBM)] * 5,
            out_specs=vmem,
            scratch_shapes=[
                pltpu.VMEM(gate_in.shape, gate_in.dtype),
                pltpu.VMEM(value_in.shape, value_in.dtype),
                pltpu.VMEM(out_gate.shape, out_gate.dtype),
                pltpu.VMEM(taps.shape, taps.dtype),
                pltpu.SMEM(skip_gain.shape, skip_gain.dtype),
                pltpu.VMEM((channels * blocks, LANES), jnp.float32),
                pltpu.VMEM(message, jnp.bfloat16),
                pltpu.VMEM(taps_message, jnp.bfloat16),
                pltpu.VMEM(message, jnp.bfloat16),
                pltpu.VMEM(taps_message, jnp.bfloat16),
                pltpu.VMEM(taps_message, jnp.float32),
                pltpu.VMEM((2, nd + n * blocks, LANES), jnp.float32),
                pltpu.VMEM(message, jnp.bfloat16),
                pltpu.VMEM(message, jnp.bfloat16),
                pltpu.VMEM((channels * blocks, LANES), jnp.float32),
                pltpu.VMEM((channels * blocks, LANES), jnp.float32),
                pltpu.VMEM((blocks, LANES), jnp.float32),
                pltpu.VMEM((m, blocks, LANES), jnp.float32),
                pltpu.SemaphoreType.DMA((5,)),
                pltpu.SemaphoreType.DMA((3, groups, n)),
                pltpu.SemaphoreType.DMA((3, groups, n)),
                pltpu.SemaphoreType.DMA((3, groups)),
                pltpu.SemaphoreType.DMA((m,)),
                pltpu.SemaphoreType.DMA((m,)),
            ],
            compiler_params=pltpu.CompilerParams(
                collective_id=0, has_side_effects=True, vmem_limit_bytes=67043328
            ),
        )(gate_in, value_in, out_gate, taps, skip_gain)

    return jax.shard_map(
        local,
        mesh=mesh,
        in_specs=(P("seq", "mp"), P("seq", "mp"), P("seq", "mp"), P("seq", "mp"), P("mp")),
        out_specs=P("seq", "mp"),
        check_vma=False,
    )
```

profile of v0, /device:TPU:0, one launch (start us, length us, event | category | flops | bytes accessed | tf_op | source)
XLA Modules:
  0.0 44.5 jit_solution(6274316428725376376)
XLA Ops:
  0.0 42.6 %shard_map.55 = bf16[1024,256]{1,0:T(8,128)(2,1)} custom-call(bf16[1024,256]{1,0:T(8,128)(2,1)} %gate_in.1, bf16[1024,256]{1,0:T(8,128)(2,1)} %value_in.1, bf16[1024,256]{1,0:T(8,128)(2,1)} %og_in.1, bf16[512,256]{1,0:T(8,128)(2,1)} %taps_in.1, f32[256]{0:T(256)} %skip_in.1), custom_call_target="tpu_custom_call" | custom-call | tf_op jit(solution)/shard_map/pallas_call | solution.py:254
  42.6 1.9 %copy.7 = bf16[1024,256]{1,0:T(8,128)(2,1)} copy(bf16[1024,256]{1,0:T(8,128)(2,1)} %shard_map.55) | data formatting | bytes 1048576
where the time goes:
time: 44.7 us; the launch traced here: 44.5 us
  Pallas kernels  42.6 us (95%)
  local copies, waits for them, and re-layouts  1.87 us (4%)
    pallas_call x1, Pallas kernels, local(): pl.pallas_call(functools.partial(kernel, cfg), out_shape=jax.ShapeDtypeSt...  42.6 us
    unnamed x1, local copies, waits for them, and re-layouts  1.87 us

commit v1 on v0

v1 whole, which is shorter than its diff:
```python
import functools

import jax
import jax.numpy as jnp
from jax import lax
from jax.experimental import pallas as pl
from jax.experimental.pallas import tpu as pltpu
from jax.sharding import PartitionSpec as P

MESH = pl.DeviceIdType.MESH
LANES = 128
TAPS, GATED, RESULT = 0, 1, 2
EPS = 1e-05


def forward_peer(me, i, n):
    if n & (n - 1) == 0:
        return me ^ (n - 1 - i)
    return lax.rem(me + 1 + i, n)


def result_peer(me, i, n):
    if n & (n - 1) or n < 4:
        return lax.rem(me + 1 + i, n)
    odd = lax.rem(me, 2)
    return jnp.where(i < me - odd, i, i + 1) ^ odd


def mp_peer(mine, k, m):
    return lax.rem(mine + k, m)


def kernel(cfg, gate_in, value_in, og_in, taps_in, skip_in, mixed, sums, gate, value, og, taps, skip, stage_h,
           stage_x, xm, hm, xr, hr, hf, xpad, rs, cr, ogt, power, powers, load_sem, send_sem, recv_sem,
           own_sem, psend_sem, precv_sem):
    n, m, channels, blocks, cl, width, groups, phases, sent_taps, hs, he, total_c = cfg
    me = lax.axis_index("seq")
    mine = lax.axis_index("mp")
    nd = hs * he
    pc = channels // phases
    per_phase = groups // phases

    def load(i, p):
        src, dst = [(taps_in, taps), (gate_in, gate), (value_in, value)][i]
        cols = slice(p * pc, (p + 1) * pc)
        return pltpu.make_async_copy(src.at[:, cols], dst.at[:, cols], load_sem.at[i, p])

    og_load = pltpu.make_async_copy(og_in, og, load_sem.at[3, 0])
    skip_load = pltpu.make_async_copy(skip_in, skip, load_sem.at[4, 0])
    for p in range(phases):
        for i in ([0, 1, 2] if sent_taps else [1, 2]):
            load(i, p).start()
    if not sent_taps:
        whole_taps = pltpu.make_async_copy(taps_in, taps, load_sem.at[0, 0])
        whole_taps.start()

    barrier = pltpu.get_barrier_semaphore()
    for i in range(n - 1):
        pl.semaphore_signal(barrier, inc=1, device_id={"seq": forward_peer(me, i, n)}, device_id_type=MESH)
    for k in range(1, m):
        pl.semaphore_signal(barrier, inc=1, device_id={"mp": mp_peer(mine, k, m)}, device_id_type=MESH)
    og_load.start()
    skip_load.start()

    def rows_of(kind, g):
        per = he if kind == TAPS else blocks
        return pl.ds(g * width * per, width * per)

    def refs(kind):
        return {TAPS: (hm, hr), GATED: (xm, xr), RESULT: (rs, cr)}[kind]

    def remote(kind, g, to):
        src, dst = refs(kind)
        rows = rows_of(kind, g)
        return pltpu.make_async_remote_copy(
            src_ref=src.at[to, rows],
            dst_ref=dst.at[me, rows],
            send_sem=send_sem.at[kind, g, to],
            recv_sem=recv_sem.at[kind, g, me],
            device_id={"seq": to},
            device_id_type=MESH,
        )

    def arrival(kind, g, whence):
        src, dst = refs(kind)
        rows = rows_of(kind, g)
        return pltpu.make_async_remote_copy(
            src_ref=src.at[whence, rows],
            dst_ref=dst.at[whence, rows],
            send_sem=send_sem.at[kind, g, whence],
            recv_sem=recv_sem.at[kind, g, whence],
            device_id={"seq": whence},
            device_id_type=MESH,
        )

    def own(kind, g):
        src, dst = refs(kind)
        rows = rows_of(kind, g)
        return pltpu.make_async_copy(src.at[me, rows], dst.at[me, rows], own_sem.at[kind, g])

    def peer(kind, i):
        return result_peer(me, i, n) if kind == RESULT else forward_peer(me, i, n)

    forward = ([TAPS] if sent_taps else []) + [GATED]

    def put(stage, dst, p, per):
        for q in range(per_phase):
            g = p * per_phase + q
            size = n * width * per
            part = stage[q * size:(q + 1) * size, :].astype(jnp.bfloat16)
            dst[:, g * width * per:(g + 1) * width * per, :] = part.reshape(n, width * per, LANES)

    for p in range(phases):
        cols = slice(p * pc, (p + 1) * pc)
        if sent_taps:
            load(0, p).wait()
            for e in range(he):
                part = taps[e * LANES:(e + 1) * LANES, cols].astype(jnp.float32)
                stage_h[pl.ds(e, pc, stride=he), :] = part.T
            put(stage_h, hm, p, he)
        load(1, p).wait()
        load(2, p).wait()
        for a in range(blocks):
            span = slice(a * LANES, (a + 1) * LANES)
            part = gate[span, cols].astype(jnp.float32) * value[span, cols].astype(jnp.float32)
            stage_x[pl.ds(a, pc, stride=blocks), :] = part.T
        put(stage_x, xm, p, blocks)
        if p == 0:
            pl.semaphore_wait(barrier, n - 1 + m - 1)
        for g in range(p * per_phase, (p + 1) * per_phase):
            for kind in forward:
                for i in range(n - 1):
                    remote(kind, g, peer(kind, i)).start()
                own(kind, g).start()

    if not sent_taps:
        whole_taps.wait()
    og_load.wait()
    skip_load.wait()
    for a in range(blocks):
        span = slice(a * LANES, (a + 1) * LANES)
        ogt[pl.ds(a, channels, stride=blocks), :] = og[span, :].astype(jnp.float32).T
    xpad[:, :nd, :] = jnp.zeros((2, nd, LANES), jnp.float32)

    lane = lax.broadcasted_iota(jnp.int32, (16, LANES), 1)
    sub = lax.broadcasted_iota(jnp.int32, (16, LANES), 0)
    total = n * blocks

    def toeplitz(c):
        lines = []
        for d in range(nd):
            source = hf if sent_taps else taps
            line = source[d // he, pl.ds(c * he + d % he, 1), :]
            line = jnp.broadcast_to(line, (16, LANES))
            lines.append(pltpu.roll(line, 0, 1, stride=1, stride_axis=0))
        zero = jnp.zeros((16, LANES), jnp.float32)
        first = []
        for d in range(nd + 1):
            here = lines[d] if d < nd else zero
            before = lines[d - 1] if d > 0 else zero
            first.append(jnp.where(lane >= sub, here, before).astype(jnp.bfloat16))
        none = jnp.zeros((16, LANES), jnp.bfloat16)
        tiles = []
        turned = [[(f if q == 0 else pltpu.roll(f, 16 * q, 1)) for q in range(8)] for f in first]
        for d in range(nd + 1):
            rows = []
            for q in range(8):
                before = turned[d - 1][q] if d > 0 else none
                rows.append(turned[d][q] if q == 0 else jnp.where(lane >= 16 * q, turned[d][q], before))
            tiles.append(jnp.concatenate(rows, axis=0))
        return tiles

    def one_pair(g, p):
        c0 = g * width + 2 * p
        start = pl.multiple_of(c0 * blocks, 2 * blocks)
        both = xr[:, pl.ds(start, 2 * blocks), :].astype(jnp.float32)
        results = []
        for e in range(2):
            rows = both[:, e * blocks:(e + 1) * blocks, :].reshape(total, LANES)
            xpad[e, nd:, :] = rows
            tiles = toeplitz(c0 + e)
            acc = rows * skip[g * n * width + me * width + 2 * p + e]
            for d in range(0, nd + 1, 2):
                ds = [d, d + 1] if d + 1 <= nd else [d]
                left = [xpad[e, nd - x:nd - x + total, :].astype(jnp.bfloat16) for x in ds]
                left = left[0] if len(ds) == 1 else jnp.concatenate(left, axis=1)
                right = tiles[d] if len(ds) == 1 else jnp.concatenate([tiles[d], tiles[d + 1]], axis=0)
                acc = acc + jnp.dot(left, right, preferred_element_type=jnp.float32)
            results.append(acc.reshape(n, blocks, LANES))
        rs[:, pl.ds(start, 2 * blocks), :] = jnp.concatenate(results, axis=1).astype(jnp.bfloat16)

    for g in range(groups):
        for kind in forward:
            own(kind, g).wait()
            for i in range(n - 1):
                arrival(kind, g, peer(kind, i)).wait_recv()
        if sent_taps:
            rows = rows_of(TAPS, g)
            hf[:, rows, :] = hr[:, rows, :].astype(jnp.float32)

        def step(p, carry):
            one_pair(g, p)
            return carry

        lax.fori_loop(0, width // 2, step, 0)
        for i in range(n - 1):
            remote(RESULT, g, peer(RESULT, i)).start()
        own(RESULT, g).start()

    power[...] = jnp.zeros_like(power)
    span = width * blocks
    for g in range(groups):
        own(RESULT, g).wait()
        for i in range(n - 1):
            arrival(RESULT, g, peer(GATED, i)).wait_recv()

        def gather(d, carry):
            rows = rows_of(RESULT, g)
            at = pl.multiple_of((g * n + d) * span, span)
            piece = ogt[pl.ds(at, span), :] * cr[d, rows, :].astype(jnp.float32)
            mixed[pl.ds(at, span), :] = piece
            square = (piece * piece).reshape(width, blocks, LANES)
            power[...] += jnp.sum(square, axis=0)
            return carry

        lax.fori_loop(0, n, gather, 0)

    def exchange(k, incoming):
        other = lax.rem(mine + m - k, m) if incoming else mp_peer(mine, k, m)
        return pltpu.make_async_remote_copy(
            src_ref=power,
            dst_ref=powers.at[other if incoming else mine],
            send_sem=psend_sem.at[k],
            recv_sem=precv_sem.at[k],
            device_id={"mp": other},
            device_id_type=MESH,
        )

    for k in range(1, m):
        exchange(k, False).start()
    for kind in forward + [RESULT]:
        for g in range(groups):
            for i in range(n - 1):
                remote(kind, g, peer(kind, i)).wait_send()
    for k in range(1, m):
        exchange(k, True).wait_recv()
    add = power[...]
    for k in range(1, m):
        add = add + powers[lax.rem(mine + m - k, m)]
    sums[...] = add
    for k in range(1, m):
        exchange(k, False).wait_send()


def finish(blocks, channels, total_c, mixed, sums, out, held, out_sem):
    scale = 1.0 / jnp.sqrt(sums[...] / total_c + EPS)

    def store(a):
        span = slice(a * LANES, (a + 1) * LANES)
        return pltpu.make_async_copy(held.at[span], out.at[span], out_sem.at[a])

    for a in range(blocks):
        part = mixed[pl.ds(a, channels, stride=blocks), :] * scale[a:a + 1, :]
        held[a * LANES:(a + 1) * LANES, :] = part.T.astype(jnp.bfloat16)
        store(a).start()
    for a in range(blocks):
        store(a).wait()


def solution(mesh):
    n, m = mesh.shape["seq"], mesh.shape["mp"]

    def local(gate_in, value_in, out_gate, filter_taps, skip_gain):
        tokens, channels = gate_in.shape
        blocks = tokens // LANES
        cl = channels // n
        width = min(cl, 8)
        groups = cl // width
        phases = channels // max(LANES, n * width)
        own_taps = filter_taps.shape[0]
        sent_taps = own_taps % LANES == 0 and (width * (own_taps // LANES)) % 16 == 0
        nd = own_taps * n // LANES
        if sent_taps:
            hs, he, taps = n, own_taps // LANES, filter_taps
        else:
            hs, he = 1, nd
            dealt = filter_taps.reshape(own_taps, groups, n, width).swapaxes(1, 2).reshape(own_taps, channels)
            moved = lax.all_to_all(dealt, "seq", split_axis=1, concat_axis=0, tiled=True)
            taps = moved.astype(jnp.float32).T.reshape(1, cl * nd, LANES)
        cfg = (n, m, channels, blocks, cl, width, groups, phases, sent_taps, hs, he, channels * m)
        message = (n, cl * blocks, LANES)
        taps_message = (n, cl * he, LANES) if sent_taps else (n, 16, LANES)
        taps_stage = (channels // phases * he, LANES) if sent_taps else (16, LANES)
        mixed, sums = pl.pallas_call(
            functools.partial(kernel, cfg),
            out_shape=[
                pltpu.VMEM((channels * blocks, LANES), jnp.float32),
                pltpu.VMEM((blocks, LANES), jnp.float32),
            ],
            in_specs=[pl.BlockSpec(memory_space=pltpu.HBM)] * 5,
            out_specs=[pl.BlockSpec(memory_space=pltpu.VMEM)] * 2,
            scratch_shapes=[
                pltpu.VMEM(gate_in.shape, gate_in.dtype),
                pltpu.VMEM(value_in.shape, value_in.dtype),
                pltpu.VMEM(out_gate.shape, out_gate.dtype),
                pltpu.VMEM(taps.shape, taps.dtype),
                pltpu.SMEM(skip_gain.shape, skip_gain.dtype),
                pltpu.VMEM(taps_stage, jnp.float32),
                pltpu.VMEM((channels // phases * blocks, LANES), jnp.float32),
                pltpu.VMEM(message, jnp.bfloat16),
                pltpu.VMEM(taps_message, jnp.bfloat16),
                pltpu.VMEM(message, jnp.bfloat16),
                pltpu.VMEM(taps_message, jnp.bfloat16),
                pltpu.VMEM(taps_message, jnp.float32),
                pltpu.VMEM((2, nd + n * blocks, LANES), jnp.float32),
                pltpu.VMEM(message, jnp.bfloat16),
                pltpu.VMEM(message, jnp.bfloat16),
                pltpu.VMEM((channels * blocks, LANES), jnp.float32),
                pltpu.VMEM((blocks, LANES), jnp.float32),
                pltpu.VMEM((m, blocks, LANES), jnp.float32),
                pltpu.SemaphoreType.DMA((5, phases)),
                pltpu.SemaphoreType.DMA((3, groups, n)),
                pltpu.SemaphoreType.DMA((3, groups, n)),
                pltpu.SemaphoreType.DMA((3, groups)),
                pltpu.SemaphoreType.DMA((m,)),
                pltpu.SemaphoreType.DMA((m,)),
            ],
            compiler_params=pltpu.CompilerParams(
                collective_id=0, has_side_effects=True, vmem_limit_bytes=32 * 1024 * 1024
            ),
        )(*(pltpu.with_memory_space_constraint(x, pltpu.HBM) for x in (gate_in, value_in, out_gate, taps, skip_gain)))
        return pl.pallas_call(
            functools.partial(finish, blocks, channels, channels * m),
            out_shape=jax.ShapeDtypeStruct((tokens, channels), jnp.bfloat16),
            in_specs=[pl.BlockSpec(memory_space=pltpu.VMEM)] * 2,
            out_specs=pl.BlockSpec(memory_space=pltpu.HBM),
            scratch_shapes=[
                pltpu.VMEM((tokens, channels), jnp.bfloat16),
                pltpu.SemaphoreType.DMA((blocks,)),
            ],
            compiler_params=pltpu.CompilerParams(vmem_limit_bytes=8 * 1024 * 1024),
        )(mixed, sums)

    return jax.shard_map(
        local,
        mesh=mesh,
        in_specs=(P("seq", "mp"), P("seq", "mp"), P("seq", "mp"), P("seq", "mp"), P("mp")),
        out_specs=P("seq", "mp"),
        check_vma=False,
    )
```

time: 44.7 us -> 42.2 us (0.944)
  local copies, waits for them, and re-layouts: 1.87 us -> 0 us
  Pallas kernels: 42.6 us -> 42 us
    unnamed x1 -> x0, local copies, waits for them, and re-layouts: 1.87 us -> none
    pallas_call x1 -> x2, Pallas kernels: 42.6 us -> 42 us  [the longest x1 41.1 us: local(): pl.pallas_call(functools.partial(kernel, cfg), out_shape=[pltpu.VMEM((cha...]
where the time goes in v1:
time: 42.2 us; the launch traced here: 42 us
  Pallas kernels  42 us (100%)
    pallas_call x1, Pallas kernels, local(): pl.pallas_call(functools.partial(kernel, cfg), out_shape=[pltpu.VMEM((cha...  41.1 us
    pallas_call x1, Pallas kernels, local(): pl.pallas_call(functools.partial(finish, blocks, channels, channels * m),...  0.97 us

profile of v1, /device:TPU:0, one launch (start us, length us, event | category | flops | bytes accessed | tf_op | source)
XLA Modules:
  0.0 42.0 jit_solution(2654945328214780870)
XLA Ops:
  0.0 41.1 %shard_map.55 = (f32[2048,128]{1,0:T(8,128)S(1)}, f32[8,128]{1,0:T(8,128)S(1)}) custom-call(bf16[1024,256]{1,0:T(8,128)(2,1)} %gate_in.1, bf16[1024,256]{1,0:T(8,128)(2,1)} %value_in.1, bf16[1024,256]{1,0:T(8,128)(2,1)} %og_in.1, bf16[512,256]{1,0:T(8,128)(2,1)} %taps_in.1, f32[256]{0:T(256)} %skip_in.1), custom_call_target="tpu_custom_call" | custom-call | tf_op jit(solution)/shard_map/pallas_call | solution.py:294
  41.1 1.0 %shard_map.56 = bf16[1024,256]{1,0:T(8,128)(2,1)} custom-call(f32[2048,128]{1,0:T(8,128)S(1)} %get-tuple-element.7.mixed, f32[8,128]{1,0:T(8,128)S(1)} %get-tuple-element.8.sums), custom_call_target="tpu_custom_call" | custom-call | tf_op jit(solution)/shard_map/pallas_call | solution.py:332

commit v2 on v1

v2 whole, which is shorter than its diff:
```python
import functools

import jax
import jax.numpy as jnp
from jax import lax
from jax.experimental import pallas as pl
from jax.experimental.pallas import tpu as pltpu
from jax.sharding import PartitionSpec as P

MESH = pl.DeviceIdType.MESH
LANES = 128
FORWARD, RESULT = 0, 1
EPS = 1e-05
MESSAGE = 16
RETURN = 16


def forward_peer(me, i, n):
    if n & (n - 1) == 0:
        return me ^ (n - 1 - i)
    return lax.rem(me + 1 + i, n)


def result_peer(me, i, n):
    if n & (n - 1) or n < 4:
        return lax.rem(me + 1 + i, n)
    odd = lax.rem(me, 2)
    return jnp.where(i < me - odd, i, i + 1) ^ odd


def mp_peer(mine, k, m):
    return lax.rem(mine + k, m)


def tap_tiles(line_of, nd):
    lane = lax.broadcasted_iota(jnp.int32, (16, LANES), 1)
    sub = lax.broadcasted_iota(jnp.int32, (16, LANES), 0)
    zero = jnp.zeros((16, LANES), jnp.float32)
    none = zero.astype(jnp.bfloat16)
    lines = []
    for d in range(nd):
        line = jnp.broadcast_to(line_of(d), (16, LANES))
        lines.append(pltpu.roll(line, 0, 1, stride=1, stride_axis=0))
    first = []
    for d in range(nd + 1):
        here = lines[d] if d < nd else zero
        before = lines[d - 1] if d > 0 else zero
        first.append(jnp.where(lane >= sub, here, before).astype(jnp.bfloat16))
    bands = [first]
    for q in range(1, 4):
        turned = [pltpu.roll(f, 16 * q, 1) for f in first]
        bands.append([jnp.where(lane >= 16 * q, turned[d], turned[d - 1] if d else none) for d in range(nd + 1)])

    def tile(step):
        d = 2 * step
        return jnp.concatenate([
            jnp.concatenate([band[d] if d <= nd else none, band[d + 1] if d + 1 <= nd else none], axis=1)
            for band in bands
        ], axis=0)

    return [tile(step) for step in range(nd // 2 + 1)]


def convolve(x, tiles, even, odd, late):
    total = x.shape[0]
    pad = even.shape[0] - total
    lane = lax.broadcasted_iota(jnp.int32, (total, LANES), 1)
    turned = pltpu.roll(x, 64, 1)
    even[pad:, :] = x
    odd[pad:, :] = turned
    x_late = even[pad - 2:pad - 2 + total, :]
    turned_late = odd[pad - 2:pad - 2 + total, :]
    even[pad:, :] = jnp.where(lane < 64, x, turned_late)
    odd[pad:, :] = jnp.where(lane < 64, turned, x_late)
    left = []
    for step in range(0, tiles.shape[0] // 64, 2):
        at = pad - 2 * step
        left.append(jnp.concatenate([even[at:at + total, :], odd[at:at + total, :]], axis=0).astype(jnp.bfloat16))
    sums = jnp.dot(jnp.concatenate(left, axis=1), tiles[...], preferred_element_type=jnp.float32)
    late[0, 8:8 + total, :] = sums[:total, LANES:]
    late[1, 8:8 + total, :] = sums[total:, LANES:]
    even_late = late[0, 7:7 + total, :]
    odd_late = late[1, 7:7 + total, :]
    straddling = pltpu.roll(sums[total:, :LANES] + odd_late, 64, 1)
    late[1, 8:8 + total, :] = straddling
    return sums[:total, :LANES] + even_late + jnp.where(lane >= 64, straddling, late[1, 7:7 + total, :])


def kernel(cfg, gate_in, value_in, og_in, taps_in, skip_in, mixed, sums, gate, value, og, taps, skip, stage_h,
           stage_x, fm, fr, hf, tiles_a, tiles_b, even, odd, late, rs, cr, ogt, power, powers,
           load_sem, send_sem, recv_sem, own_sem, psend_sem, precv_sem):
    n, m, channels, blocks, cl, width, groups, phases, returns, sent_taps, hs, he, total_c = cfg
    me = lax.axis_index("seq")
    mine = lax.axis_index("mp")
    nd = hs * he
    pc = channels // phases
    sent = he if sent_taps else 0
    per = sent + blocks
    per_phase = groups // phases

    def load(i, p):
        src, dst = [(taps_in, taps), (gate_in, gate), (value_in, value)][i]
        cols = slice(p * pc, (p + 1) * pc)
        return pltpu.make_async_copy(src.at[:, cols], dst.at[:, cols], load_sem.at[i, p])

    og_load = pltpu.make_async_copy(og_in, og, load_sem.at[3, 0])
    skip_load = pltpu.make_async_copy(skip_in, skip, load_sem.at[4, 0])
    for p in range(phases):
        for i in ([0, 1, 2] if sent_taps else [1, 2]):
            load(i, p).start()
    if not sent_taps:
        whole_taps = pltpu.make_async_copy(taps_in, taps, load_sem.at[0, 0])
        whole_taps.start()

    barrier = pltpu.get_barrier_semaphore()
    for i in range(n - 1):
        pl.semaphore_signal(barrier, inc=1, device_id={"seq": forward_peer(me, i, n)}, device_id_type=MESH)
    for k in range(1, m):
        pl.semaphore_signal(barrier, inc=1, device_id={"mp": mp_peer(mine, k, m)}, device_id_type=MESH)
    og_load.start()
    skip_load.start()

    def rows_of(kind, g):
        if kind == RESULT:
            return pl.ds(g * returns * blocks, returns * blocks)
        return pl.ds(g * width * per, width * per)

    refs = {FORWARD: (fm, fr), RESULT: (rs, cr)}

    def remote(kind, g, to):
        src, dst = refs[kind]
        rows = rows_of(kind, g)
        return pltpu.make_async_remote_copy(
            src_ref=src.at[to, rows],
            dst_ref=dst.at[me, rows],
            send_sem=send_sem.at[kind, g, to],
            recv_sem=recv_sem.at[kind, g, me],
            device_id={"seq": to},
            device_id_type=MESH,
        )

    def arrival(kind, g, whence):
        src, dst = refs[kind]
        rows = rows_of(kind, g)
        return pltpu.make_async_remote_copy(
            src_ref=src.at[whence, rows],
            dst_ref=dst.at[whence, rows],
            send_sem=send_sem.at[kind, g, whence],
            recv_sem=recv_sem.at[kind, g, whence],
            device_id={"seq": whence},
            device_id_type=MESH,
        )

    def own(kind, g):
        src, dst = refs[kind]
        rows = rows_of(kind, g)
        return pltpu.make_async_copy(src.at[me, rows], dst.at[me, rows], own_sem.at[kind, g])

    everyone = [forward_peer(me, i, n) for i in range(n - 1)]
    in_turn = [result_peer(me, i, n) for i in range(n - 1)]

    def put(stage, p, offset, rows):
        for q in range(per_phase):
            g = p * per_phase + q
            size = n * width * rows
            part = stage[q * size:(q + 1) * size, :].astype(jnp.bfloat16)
            at = g * width * per + offset
            fm[:, at:at + width * rows, :] = part.reshape(n, width * rows, LANES)

    def send_forward(g):
        for to in everyone:
            remote(FORWARD, g, to).start()
        own(FORWARD, g).start()

    for p in range(phases):
        cols = slice(p * pc, (p + 1) * pc)
        if sent_taps:
            load(0, p).wait()
            for e in range(he):
                part = taps[e * LANES:(e + 1) * LANES, cols].astype(jnp.float32)
                stage_h[pl.ds(e, pc, stride=he), :] = part.T
            put(stage_h, p, 0, he)
        load(1, p).wait()
        load(2, p).wait()
        for a in range(blocks):
            span = slice(a * LANES, (a + 1) * LANES)
            part = gate[span, cols].astype(jnp.float32) * value[span, cols].astype(jnp.float32)
            stage_x[pl.ds(a, pc, stride=blocks), :] = part.T
        put(stage_x, p, width * sent, blocks)
        if p == 0:
            pl.semaphore_wait(barrier, n - 1 + m - 1)
        for g in range(p * per_phase, (p + 1) * per_phase):
            send_forward(g)

    if not sent_taps:
        whole_taps.wait()
    og_load.wait()
    skip_load.wait()
    for a in range(blocks):
        span = slice(a * LANES, (a + 1) * LANES)
        ogt[pl.ds(a, channels, stride=blocks), :] = og[span, :].astype(jnp.float32).T
    total = n * blocks
    pad = even.shape[1] - total
    even[:, :pad, :] = jnp.zeros((4, pad, LANES), jnp.float32)
    odd[:, :pad, :] = jnp.zeros((4, pad, LANES), jnp.float32)
    late[:, :, :8, :] = jnp.zeros((4, 2, 8, LANES), jnp.float32)
    reach = 64 * (nd // 2 + 1)
    for tiles in (tiles_a, tiles_b):
        if tiles.shape[1] > reach:
            tiles[:, reach:, :] = jnp.zeros((2, tiles.shape[1] - reach, 2 * LANES), jnp.bfloat16)

    filters = hf if sent_taps else taps

    def build(pair, tiles):
        for e in range(2):
            def line_of(d):
                return filters[d // he, pl.ds((2 * pair + e) * he + d % he, 1), :]

            for i, tile in enumerate(tap_tiles(line_of, nd)):
                tiles[e, 64 * i:64 * (i + 1), :] = tile

    def apply(g, p, tiles, half):
        pair = g * (width // 2) + p
        begin = pl.multiple_of(g * width * per + width * sent + 2 * blocks * p, 16)
        start = pl.multiple_of(2 * blocks * pair, 16)
        both = fr[:, pl.ds(begin, 2 * blocks), :].astype(jnp.float32)
        results = []
        for e in range(2):
            x = both[:, e * blocks:(e + 1) * blocks, :].reshape(total, LANES)
            at = 2 * half + e
            y = convolve(x, tiles.at[e], even.at[at], odd.at[at], late.at[at])
            y = y + x * skip[g * n * width + me * width + 2 * p + e]
            results.append(y.reshape(n, blocks, LANES))
        rs[:, pl.ds(start, 2 * blocks), :] = jnp.concatenate(results, axis=1).astype(jnp.bfloat16)

    last = width // 2 - 1
    per_group = width // returns
    for g in range(groups):
        own(FORWARD, g).wait()
        for whence in everyone:
            arrival(FORWARD, g, whence).wait_recv()
        if sent_taps:
            rows = pl.ds(g * width * per, width * sent)
            hf[:, g * width * he:(g + 1) * width * he, :] = fr[:, rows, :].astype(jnp.float32)
        first = g * (width // 2)
        build(first, tiles_a)

        def step(i, carry):
            apply(g, 2 * i, tiles_a, 0)
            build(first + 2 * i + 1, tiles_b)
            apply(g, 2 * i + 1, tiles_b, 1)
            build(first + jnp.minimum(2 * i + 2, last), tiles_a)
            return carry

        for r in range(per_group):
            lax.fori_loop(r * returns // 4, (r + 1) * returns // 4, step, 0)
            for to in in_turn:
                remote(RESULT, g * per_group + r, to).start()
            own(RESULT, g * per_group + r).start()

    power[...] = jnp.zeros_like(power)
    span = returns * blocks
    for g in range(groups * per_group):
        own(RESULT, g).wait()
        for whence in everyone:
            arrival(RESULT, g, whence).wait_recv()

        def gather(d, carry):
            at = ((g // per_group) * n + d) * width * blocks + (g % per_group) * span
            at = pl.multiple_of(at, span)
            piece = ogt[pl.ds(at, span), :] * cr[d, rows_of(RESULT, g), :].astype(jnp.float32)
            mixed[pl.ds(at, span), :] = piece
            square = (piece * piece).reshape(returns, blocks, LANES)
            power[...] += jnp.sum(square, axis=0)
            return carry

        lax.fori_loop(0, n, gather, 0)

    def exchange(k, incoming):
        other = lax.rem(mine + m - k, m) if incoming else mp_peer(mine, k, m)
        return pltpu.make_async_remote_copy(
            src_ref=power,
            dst_ref=powers.at[other if incoming else mine],
            send_sem=psend_sem.at[k],
            recv_sem=precv_sem.at[k],
            device_id={"mp": other},
            device_id_type=MESH,
        )

    for k in range(1, m):
        exchange(k, False).start()
    for g in range(groups):
        for to in everyone:
            remote(FORWARD, g, to).wait_send()
    for g in range(groups * per_group):
        for to in in_turn:
            remote(RESULT, g, to).wait_send()
    for k in range(1, m):
        exchange(k, True).wait_recv()
    add = power[...]
    for k in range(1, m):
        add = add + powers[lax.rem(mine + m - k, m)]
    sums[...] = add
    for k in range(1, m):
        exchange(k, False).wait_send()


def finish(blocks, channels, total_c, mixed, sums, out, held, out_sem):
    scale = 1.0 / jnp.sqrt(sums[...] / total_c + EPS)

    def store(a):
        span = slice(a * LANES, (a + 1) * LANES)
        return pltpu.make_async_copy(held.at[span], out.at[span], out_sem.at[a])

    for a in range(blocks):
        part = mixed[pl.ds(a, channels, stride=blocks), :] * scale[a:a + 1, :]
        held[a * LANES:(a + 1) * LANES, :] = part.T.astype(jnp.bfloat16)
        store(a).start()
    for a in range(blocks):
        store(a).wait()


def solution(mesh):
    n, m = mesh.shape["seq"], mesh.shape["mp"]

    def local(gate_in, value_in, out_gate, filter_taps, skip_gain):
        tokens, channels = gate_in.shape
        blocks = tokens // LANES
        cl = channels // n
        width = min(cl, MESSAGE)
        groups = cl // width
        phases = channels // max(LANES, n * width)
        own_taps = filter_taps.shape[0]
        sent_taps = own_taps % LANES == 0 and (width * (own_taps // LANES)) % 16 == 0
        nd = own_taps * n // LANES
        if sent_taps:
            hs, he, taps = n, own_taps // LANES, filter_taps
        else:
            hs, he = 1, nd
            dealt = filter_taps.reshape(own_taps, groups, n, width).swapaxes(1, 2).reshape(own_taps, channels)
            moved = lax.all_to_all(dealt, "seq", split_axis=1, concat_axis=0, tiled=True)
            taps = moved.astype(jnp.float32).T.reshape(1, cl * nd, LANES)
        returns = min(width, RETURN)
        pad = -(-(nd + 2) // 8) * 8
        depth = (nd // 2 + 2) // 2 * 128
        cfg = (n, m, channels, blocks, cl, width, groups, phases, returns, sent_taps, hs, he, channels * m)
        message = (n, cl * blocks, LANES)
        taps_message = (n, cl * he, LANES) if sent_taps else (1, 16, LANES)
        both_message = (n, cl * (blocks + (he if sent_taps else 0)), LANES)
        taps_stage = (channels // phases * he, LANES) if sent_taps else (16, LANES)
        mixed, sums = pl.pallas_call(
            functools.partial(kernel, cfg),
            out_shape=[
                pltpu.VMEM((channels * blocks, LANES), jnp.float32),
                pltpu.VMEM((blocks, LANES), jnp.float32),
            ],
            in_specs=[pl.BlockSpec(memory_space=pltpu.HBM)] * 5,
            out_specs=[pl.BlockSpec(memory_space=pltpu.VMEM)] * 2,
            scratch_shapes=[
                pltpu.VMEM(gate_in.shape, gate_in.dtype),
                pltpu.VMEM(value_in.shape, value_in.dtype),
                pltpu.VMEM(out_gate.shape, out_gate.dtype),
                pltpu.VMEM(taps.shape, taps.dtype),
                pltpu.SMEM(skip_gain.shape, skip_gain.dtype),
                pltpu.VMEM(taps_stage, jnp.float32),
                pltpu.VMEM((channels // phases * blocks, LANES), jnp.float32),
                pltpu.VMEM(both_message, jnp.bfloat16),
                pltpu.VMEM(both_message, jnp.bfloat16),
                pltpu.VMEM(taps_message, jnp.float32),
                pltpu.VMEM((2, depth, 2 * LANES), jnp.bfloat16),
                pltpu.VMEM((2, depth, 2 * LANES), jnp.bfloat16),
                pltpu.VMEM((4, pad + n * blocks, LANES), jnp.float32),
                pltpu.VMEM((4, pad + n * blocks, LANES), jnp.float32),
                pltpu.VMEM((4, 2, 8 + n * blocks, LANES), jnp.float32),
                pltpu.VMEM(message, jnp.bfloat16),
                pltpu.VMEM(message, jnp.bfloat16),
                pltpu.VMEM((channels * blocks, LANES), jnp.float32),
                pltpu.VMEM((blocks, LANES), jnp.float32),
                pltpu.VMEM((m, blocks, LANES), jnp.float32),
                pltpu.SemaphoreType.DMA((5, phases)),
                pltpu.SemaphoreType.DMA((2, cl // returns, n)),
                pltpu.SemaphoreType.DMA((2, cl // returns, n)),
                pltpu.SemaphoreType.DMA((2, cl // returns)),
                pltpu.SemaphoreType.DMA((m,)),
                pltpu.SemaphoreType.DMA((m,)),
            ],
            compiler_params=pltpu.CompilerParams(
                collective_id=0, has_side_effects=True, vmem_limit_bytes=32 * 1024 * 1024
            ),
        )(*(pltpu.with_memory_space_constraint(x, pltpu.HBM) for x in (gate_in, value_in, out_gate, taps, skip_gain)))
        return pl.pallas_call(
            functools.partial(finish, blocks, channels, channels * m),
            out_shape=jax.ShapeDtypeStruct((tokens, channels), jnp.bfloat16),
            in_specs=[pl.BlockSpec(memory_space=pltpu.VMEM)] * 2,
            out_specs=pl.BlockSpec(memory_space=pltpu.HBM),
            scratch_shapes=[
                pltpu.VMEM((tokens, channels), jnp.bfloat16),
                pltpu.SemaphoreType.DMA((blocks,)),
            ],
            compiler_params=pltpu.CompilerParams(vmem_limit_bytes=8 * 1024 * 1024),
        )(mixed, sums)

    return jax.shard_map(
        local,
        mesh=mesh,
        in_specs=(P("seq", "mp"), P("seq", "mp"), P("seq", "mp"), P("seq", "mp"), P("mp")),
        out_specs=P("seq", "mp"),
        check_vma=False,
    )
```

time: 42.2 us -> 39.4 us (0.934)
  Pallas kernels: 42 us -> 39.2 us
    pallas_call x1, Pallas kernels: 41.1 us -> 38.3 us  [local(): pl.pallas_call(functools.partial(kernel, cfg), out_shape=[pltpu.VMEM((cha...]
where the time goes in v2:
time: 39.4 us; the launch traced here: 39.2 us
  Pallas kernels  39.2 us (99%)
    pallas_call x1, Pallas kernels, local(): pl.pallas_call(functools.partial(kernel, cfg), out_shape=[pltpu.VMEM((cha...  38.3 us
    pallas_call x1, Pallas kernels, local(): pl.pallas_call(functools.partial(finish, blocks, channels, channels * m),...  0.97 us

profile of v2, /device:TPU:0, one launch (start us, length us, event | category | flops | bytes accessed | tf_op | source)
XLA Modules:
  0.0 39.2 jit_solution(6098018051106510375)
XLA Ops:
  0.0 38.3 %shard_map.55 = (f32[2048,128]{1,0:T(8,128)S(1)}, f32[8,128]{1,0:T(8,128)S(1)}) custom-call(bf16[1024,256]{1,0:T(8,128)(2,1)} %gate_in.1, bf16[1024,256]{1,0:T(8,128)(2,1)} %value_in.1, bf16[1024,256]{1,0:T(8,128)(2,1)} %og_in.1, bf16[512,256]{1,0:T(8,128)(2,1)} %taps_in.1, f32[256]{0:T(256)} %skip_in.1), custom_call_target="tpu_custom_call" | custom-call | tf_op jit(solution)/shard_map/pallas_call | solution.py:351
  38.3 1.0 %shard_map.56 = bf16[1024,256]{1,0:T(8,128)(2,1)} custom-call(f32[2048,128]{1,0:T(8,128)S(1)} %get-tuple-element.7.mixed, f32[8,128]{1,0:T(8,128)S(1)} %get-tuple-element.8.sums), custom_call_target="tpu_custom_call" | custom-call | tf_op jit(solution)/shard_map/pallas_call | solution.py:391

commit v3 on v2

--- a/solution.py
+++ b/solution.py
@@ -86,9 +86,9 @@
     return sums[:total, :LANES] + even_late + jnp.where(lane >= 64, straddling, late[1, 7:7 + total, :])
 
 
-def kernel(cfg, gate_in, value_in, og_in, taps_in, skip_in, mixed, sums, gate, value, og, taps, skip, stage_h,
+def kernel(cfg, gate_in, value_in, og_in, taps_in, skip_in, turned, sums, gate, value, og, taps, skip, stage_h,
            stage_x, fm, fr, hf, tiles_a, tiles_b, even, odd, late, rs, cr, ogt, power, powers,
-           load_sem, send_sem, recv_sem, own_sem, psend_sem, precv_sem):
+           load_sem, send_sem, recv_sem, own_sem, psend_sem, precv_sem, mixed):
     n, m, channels, blocks, cl, width, groups, phases, returns, sent_taps, hs, he, total_c = cfg
     me = lax.axis_index("seq")
     mine = lax.axis_index("mp")
@@ -171,6 +171,8 @@
         for to in everyone:
             remote(FORWARD, g, to).start()
         own(FORWARD, g).start()
+
+    outer = lax.rem(mine, 2) == 0
 
     for p in range(phases):
         cols = slice(p * pc, (p + 1) * pc)
@@ -190,7 +192,10 @@
         if p == 0:
             pl.semaphore_wait(barrier, n - 1 + m - 1)
         for g in range(p * per_phase, (p + 1) * per_phase):
-            send_forward(g)
+            if g == 0:
+                send_forward(g)
+            else:
+                pl.when(outer)(functools.partial(send_forward, g))
 
     if not sent_taps:
         whole_taps.wait()
@@ -239,6 +244,8 @@
         own(FORWARD, g).wait()
         for whence in everyone:
             arrival(FORWARD, g, whence).wait_recv()
+        if g + 1 < groups:
+            pl.when(jnp.logical_not(outer))(functools.partial(send_forward, g + 1))
         if sent_taps:
             rows = pl.ds(g * width * per, width * sent)
             hf[:, g * width * he:(g + 1) * width * he, :] = fr[:, rows, :].astype(jnp.float32)
@@ -261,20 +268,19 @@
     power[...] = jnp.zeros_like(power)
     span = returns * blocks
     for g in range(groups * per_group):
-        own(RESULT, g).wait()
-        for whence in everyone:
-            arrival(RESULT, g, whence).wait_recv()
-
-        def gather(d, carry):
+        def gather(d):
             at = ((g // per_group) * n + d) * width * blocks + (g % per_group) * span
             at = pl.multiple_of(at, span)
             piece = ogt[pl.ds(at, span), :] * cr[d, rows_of(RESULT, g), :].astype(jnp.float32)
             mixed[pl.ds(at, span), :] = piece
             square = (piece * piece).reshape(returns, blocks, LANES)
             power[...] += jnp.sum(square, axis=0)
-            return carry
-
-        lax.fori_loop(0, n, gather, 0)
+
+        own(RESULT, g).wait()
+        gather(me)
+        for whence in reversed(everyone):
+            arrival(RESULT, g, whence).wait_recv()
+            gather(whence)
 
     def exchange(k, incoming):
         other = lax.rem(mine + m - k, m) if incoming else mp_peer(mine, k, m)
@@ -289,6 +295,8 @@
 
     for k in range(1, m):
         exchange(k, False).start()
+    for a in range(blocks):
+        turned[a * LANES:(a + 1) * LANES, :] = mixed[pl.ds(a, channels, stride=blocks), :].T
     for g in range(groups):
         for to in everyone:
             remote(FORWARD, g, to).wait_send()
@@ -305,7 +313,7 @@
         exchange(k, False).wait_send()
 
 
-def finish(blocks, channels, total_c, mixed, sums, out, held, out_sem):
+def finish(blocks, channels, total_c, turned, sums, out, held, out_sem):
     scale = 1.0 / jnp.sqrt(sums[...] / total_c + EPS)
 
     def store(a):
@@ -313,8 +321,9 @@
         return pltpu.make_async_copy(held.at[span], out.at[span], out_sem.at[a])
 
     for a in range(blocks):
-        part = mixed[pl.ds(a, channels, stride=blocks), :] * scale[a:a + 1, :]
-        held[a * LANES:(a + 1) * LANES, :] = part.T.astype(jnp.bfloat16)
+        span = slice(a * LANES, (a + 1) * LANES)
+        column = jnp.broadcast_to(scale[a:a + 1, :], (LANES, LANES)).T
+        held[span, :] = (turned[span, :] * jnp.concatenate([column] * (channels // LANES), axis=1)).astype(jnp.bfloat16)
         store(a).start()
     for a in range(blocks):
         store(a).wait()
@@ -351,7 +360,7 @@
         mixed, sums = pl.pallas_call(
             functools.partial(kernel, cfg),
             out_shape=[
-                pltpu.VMEM((channels * blocks, LANES), jnp.float32),
+                pltpu.VMEM((tokens, channels), jnp.float32),
                 pltpu.VMEM((blocks, LANES), jnp.float32),
             ],
             in_specs=[pl.BlockSpec(memory_space=pltpu.HBM)] * 5,
@@ -383,6 +392,7 @@
                 pltpu.SemaphoreType.DMA((2, cl // returns)),
                 pltpu.SemaphoreType.DMA((m,)),
                 pltpu.SemaphoreType.DMA((m,)),
+                pltpu.VMEM((channels * blocks, LANES), jnp.float32),
             ],
             compiler_params=pltpu.CompilerParams(
                 collective_id=0, has_side_effects=True, vmem_limit_bytes=32 * 1024 * 1024

time: 39.4 us -> 38.9 us (0.987)
  Pallas kernels: 39.2 us -> 38.8 us
    pallas_call x1, Pallas kernels: 38.3 us -> 37.8 us  [local(): pl.pallas_call(functools.partial(kernel, cfg), out_shape=[pltpu.VMEM((tok...]
where the time goes in v3:
time: 38.9 us; the launch traced here: 38.8 us
  Pallas kernels  38.8 us (100%)
    pallas_call x1, Pallas kernels, local(): pl.pallas_call(functools.partial(kernel, cfg), out_shape=[pltpu.VMEM((tok...  37.8 us
    pallas_call x1, Pallas kernels, local(): pl.pallas_call(functools.partial(finish, blocks, channels, channels * m),...  0.97 us

profile of v3, /device:TPU:0, one launch (start us, length us, event | category | flops | bytes accessed | tf_op | source)
XLA Modules:
  0.0 38.8 jit_solution(13701529032650737424)
XLA Ops:
  0.0 37.8 %shard_map.55 = (f32[1024,256]{1,0:T(8,128)S(1)}, f32[8,128]{1,0:T(8,128)S(1)}) custom-call(bf16[1024,256]{1,0:T(8,128)(2,1)} %gate_in.1, bf16[1024,256]{1,0:T(8,128)(2,1)} %value_in.1, bf16[1024,256]{1,0:T(8,128)(2,1)} %og_in.1, bf16[512,256]{1,0:T(8,128)(2,1)} %taps_in.1, f32[256]{0:T(256)} %skip_in.1), custom_call_target="tpu_custom_call" | custom-call | tf_op jit(solution)/shard_map/pallas_call | solution.py:360
  37.8 1.0 %shard_map.56 = bf16[1024,256]{1,0:T(8,128)(2,1)} custom-call(f32[1024,256]{1,0:T(8,128)S(1)} %get-tuple-element.7.turned, f32[8,128]{1,0:T(8,128)S(1)} %get-tuple-element.8.sums), custom_call_target="tpu_custom_call" | custom-call | tf_op jit(solution)/shard_map/pallas_call | solution.py:401

commit v4 on v3

--- a/solution.py
+++ b/solution.py
@@ -172,7 +172,7 @@
             remote(FORWARD, g, to).start()
         own(FORWARD, g).start()
 
-    outer = lax.rem(mine, 2) == 0
+    outer = (lax.rem(mine, 2) == 0) & ((me < n // 4) | (me >= n - n // 4))
 
     for p in range(phases):
         cols = slice(p * pc, (p + 1) * pc)

time: 38.9 us -> 38.9 us (level)
  no operation moved by 1% of the time
where the time goes in v4:
time: 38.9 us; the launch traced here: 38.8 us
  Pallas kernels  38.8 us (100%)
    pallas_call x1, Pallas kernels, local(): pl.pallas_call(functools.partial(kernel, cfg), out_shape=[pltpu.VMEM((tok...  37.8 us
    pallas_call x1, Pallas kernels, local(): pl.pallas_call(functools.partial(finish, blocks, channels, channels * m),...  0.97 us

profile of v4, /device:TPU:0, one launch (start us, length us, event | category | flops | bytes accessed | tf_op | source)
XLA Modules:
  0.0 38.8 jit_solution(11141534842035015266)
XLA Ops:
  0.0 37.8 %shard_map.55 = (f32[1024,256]{1,0:T(8,128)S(1)}, f32[8,128]{1,0:T(8,128)S(1)}) custom-call(bf16[1024,256]{1,0:T(8,128)(2,1)} %gate_in.1, bf16[1024,256]{1,0:T(8,128)(2,1)} %value_in.1, bf16[1024,256]{1,0:T(8,128)(2,1)} %og_in.1, bf16[512,256]{1,0:T(8,128)(2,1)} %taps_in.1, f32[256]{0:T(256)} %skip_in.1), custom_call_target="tpu_custom_call" | custom-call | tf_op jit(solution)/shard_map/pallas_call | solution.py:360
  37.8 1.0 %shard_map.56 = bf16[1024,256]{1,0:T(8,128)(2,1)} custom-call(f32[1024,256]{1,0:T(8,128)S(1)} %get-tuple-element.7.turned, f32[8,128]{1,0:T(8,128)S(1)} %get-tuple-element.8.sums), custom_call_target="tpu_custom_call" | custom-call | tf_op jit(solution)/shard_map/pallas_call | solution.py:401
